TPU v7x, 256 devices: a whole 4x4x8 slice. The times are simulated.
256 devices in a mesh: tm: 128 (over x_hi, y, z, core), pb: 2 (over x_lo).
Axes of the slice: x: 4 (x_hi: 2, x_lo: 2; x = x_hi * 2 + x_lo), y: 4, z: 8, core: 2. Of those that a mesh axis runs over, the one named last changes fastest.
Arguments:
- queries: bfloat16 [32768, 768], P(('tm', 'pb')), may hold values from -64 to 64
- corpus: bfloat16 [2097152, 768], P(('tm', 'pb')), may hold values from -40 to 40
- window_start: int32 [32768, 2], P(('tm', 'pb')), may hold values from 0 to 2097150, as said below
- window_end: int32 [32768, 2], P(('tm', 'pb')), may hold values from 2 to 2097152, as said below
Outputs:
- pooled: bfloat16 [32768, 2, 768], P(('tm', 'pb'))
- log_mass: float32 [32768, 2], P(('tm', 'pb'))
- mean_score: float32 [32768, 2], P(('tm', 'pb'))
Inputs may be any that keep to these rules, and one draw needn't show every extreme that they name: `window_start`: for query q both windows are nonempty and lie within documents (q // 128 - 1) * 8192 to (q // 128 + 2) * 8192 - 1, that is the time block of q and the blocks just before and after it. window_end[q, w] > window_start[q, w], and window_end[q, w] <= (q // 128 + 2) * 8192.
All inputs are finite; a program needn't handle non-finite values.
Results may differ from a plain program's by a relative error of at most 0.0051.
Values may be sent and summed in bfloat16 or wider, within the bound.
A program may use at most 128 MiB of HBM per device.

v0:
```python
from functools import reduce
import math

import jax
import jax.numpy as jnp
from jax import lax
from jax.sharding import PartitionSpec as P

NEG_FILL = -1e30
SCORE_SCALE = 3.0


def shifted(shard, axis, by):
    size = lax.axis_size(axis)
    pairs = [(i, i + by) for i in range(size) if 0 <= i + by < size]
    return lax.ppermute(shard, axis, pairs)


def block_state(query_rows, first_doc, stop_doc, block, start_doc):
    scores = lax.dot_general(
        query_rows, block, (((1,), (1,)), ((), ())), preferred_element_type=jnp.float32
    )
    scores = scores * (SCORE_SCALE / math.sqrt(block.shape[1]))
    doc_index = start_doc + jnp.arange(block.shape[0], dtype=jnp.int32)
    maxima, totals, parts, score_sums, counts = ([], [], [], [], [])
    for window in range(2):
        inside = (doc_index[None, :] >= first_doc[:, window : window + 1]) & (
            doc_index[None, :] < stop_doc[:, window : window + 1]
        )
        window_max = jnp.max(jnp.where(inside, scores, NEG_FILL), axis=1)
        weights = jnp.where(inside, jnp.exp(scores - window_max[:, None]), 0.0)
        maxima.append(window_max)
        totals.append(jnp.sum(weights, axis=1))
        parts.append(
            jnp.dot(weights.astype(jnp.bfloat16), block, preferred_element_type=jnp.float32).astype(
                jnp.bfloat16
            )
        )
        score_sums.append(jnp.sum(jnp.where(inside, scores, 0.0), axis=1))
        counts.append(jnp.sum(inside.astype(jnp.float32), axis=1))
    return (
        jnp.stack(maxima, 1),
        jnp.stack(totals, 1),
        jnp.stack(parts, 1),
        jnp.stack(score_sums, 1),
        jnp.stack(counts, 1),
    )


def combine(states):
    tops = [jnp.where(member[4] > 0, member[0], NEG_FILL) for member in states]
    overall = reduce(jnp.maximum, tops)
    rescale = [jnp.exp(value - overall) for value in tops]
    denominator = reduce(jnp.add, [factor * member[1] for factor, member in zip(rescale, states)])
    weighted = reduce(
        jnp.add,
        [
            factor[..., None] * member[2].astype(jnp.float32)
            for factor, member in zip(rescale, states)
        ],
    )
    pooled = (weighted / denominator[..., None]).astype(jnp.bfloat16)
    log_mass = overall + jnp.log(denominator)
    mean_score = reduce(jnp.add, [member[3] for member in states]) / reduce(
        jnp.add, [member[4] for member in states]
    )
    return (pooled, log_mass, mean_score)


def local(queries, corpus, window_start, window_end):
    block_rows = corpus.shape[0]
    position = lax.axis_index(("tm", "pb"))
    start_doc = position * block_rows
    own_state = block_state(queries, window_start, window_end, corpus, start_doc)
    prior_rows, prior_first, prior_stop = shifted(
        (queries, window_start, window_end), ("tm", "pb"), 1
    )
    next_rows, next_first, next_stop = shifted(
        (queries, window_start, window_end), ("tm", "pb"), -1
    )
    for_prior = block_state(prior_rows, prior_first, prior_stop, corpus, start_doc)
    for_next = block_state(next_rows, next_first, next_stop, corpus, start_doc)
    upper_stats = shifted(
        (for_prior[0], for_prior[1], for_prior[3], for_prior[4]), ("tm", "pb"), -1
    )
    upper_parts = shifted(for_prior[2], ("tm", "pb"), -1)
    lower_stats = shifted((for_next[0], for_next[1], for_next[3], for_next[4]), ("tm", "pb"), 1)
    lower_parts = shifted(for_next[2], ("tm", "pb"), 1)
    upper_state = (upper_stats[0], upper_stats[1], upper_parts, upper_stats[2], upper_stats[3])
    lower_state = (lower_stats[0], lower_stats[1], lower_parts, lower_stats[2], lower_stats[3])
    return combine([lower_state, own_state, upper_state])


def solution(mesh):
    placed = (
        P(("tm", "pb"), None),
        P(("tm", "pb"), None),
        P(("tm", "pb"), None),
        P(("tm", "pb"), None),
    )
    return jax.shard_map(
        local,
        mesh=mesh,
        in_specs=placed,
        out_specs=(P(("tm", "pb"), None, None), P(("tm", "pb"), None), P(("tm", "pb"), None)),
        check_vma=False,
    )
```

profile of v0, /device:TPU:4, one launch (start us, length us, event | category | flops | bytes accessed | tf_op | source)
XLA Modules:
  0.0 138.3 jit_solution(9002093593626485213)
XLA Ops:
  0.6 3.1 %collective-permute-start.5 = (s32[128,2]{0,1:T(2,128)}, s32[128,2]{0,1:T(2,128)S(1)}, u32[]{:S(2)}, u32[]{:S(2)}) collective-permute-start(s32[128,2]{0,1:T(2,128)} %param.6), channel_id=1, source_target_pairs={{0,1},{1,2},{2,3},{3,4},{4,5},{5,6},{6,7},{7,8},{8,9},{9,10},{10,1... | collective-permute-start | bytes 3080 | tf_op jit(solution)/shard_map/ppermute | solution.py:16
  3.7 8.4 %collective-permute-start = (s32[128,2]{0,1:T(2,128)}, s32[128,2]{0,1:T(2,128)S(1)}, u32[]{:S(2)}, u32[]{:S(2)}) collective-permute-start(s32[128,2]{0,1:T(2,128)} %param.6), channel_id=1, source_target_pairs={{1,0},{2,1},{3,2},{4,3},{5,4},{6,5},{7,6},{8,7},{9,8},{10,9},{11,1... | collective-permute-start | bytes 3080 | tf_op jit(solution)/shard_map/ppermute | solution.py:16
  12.2 3.4 %collective-permute-start.1 = (s32[128,2]{0,1:T(2,128)}, s32[128,2]{0,1:T(2,128)S(1)}, u32[]{:S(2)}, u32[]{:S(2)}) collective-permute-start(s32[128,2]{0,1:T(2,128)} %param.7), channel_id=1, source_target_pairs={{1,0},{2,1},{3,2},{4,3},{5,4},{6,5},{7,6},{8,7},{9,8},{10,9},{11,1... | collective-permute-start | bytes 3080 | tf_op jit(solution)/shard_map/ppermute | solution.py:16
  15.6 2.5 %collective-permute-start.6 = (s32[128,2]{0,1:T(2,128)}, s32[128,2]{0,1:T(2,128)S(1)}, u32[]{:S(2)}, u32[]{:S(2)}) collective-permute-start(s32[128,2]{0,1:T(2,128)} %param.7), channel_id=1, source_target_pairs={{0,1},{1,2},{2,3},{3,4},{4,5},{5,6},{6,7},{7,8},{8,9},{9,10},{10,1... | collective-permute-start | bytes 3080 | tf_op jit(solution)/shard_map/ppermute | solution.py:16
  18.0 7.3 %collective-permute-start.3 = (bf16[128,768]{1,0:T(8,128)(2,1)}, bf16[128,768]{1,0:T(8,128)(2,1)S(1)}, u32[]{:S(2)}, u32[]{:S(2)}) collective-permute-start(bf16[128,768]{1,0:T(8,128)(2,1)} %param.4), channel_id=1, source_target_pairs={{1,0},{2,1},{3,2},{4,3},{5,4},{6,5},{7,6},{8,7},{9,8},{10,9},{11,1... | collective-permute-start | bytes 589832 | tf_op jit(solution)/shard_map/ppermute | solution.py:16
  25.4 0.8 slice_bitcast_fusion.4
  26.1 0.0 copy-start
  26.1 11.7 %select_reduce_fusion.9 = (f32[128]{0:T(128)S(1)}, f32[128]{0:T(128)S(1)}, f32[128]{0:T(128)S(1)}, f32[128,8192]{1,0:T(8,128)}) fusion(s32[128]{0:T(128)S(1)} %get-tuple-element.64, s32[128]{0:T(128)S(1)} %get-tuple-element.67, s32[8192]{0:T(1024)S(1)} %iota_add_fusion, s32[128]{0:T(128)S(1)} %get-tuple-element.63, s32[128]{0:T(128)S(1)} %get-tuple-element.68, ...), kind=kOutput, calls=%fused_computation.20 | convolution fusion | flops 1624243840 | bytes 17010176 | tf_op jit(solution)/shard_map/dot_general | solution.py:20
  37.8 4.5 %fusion.60 = bf16[128,1,768]{2,0,1:T(8,128)(2,1)S(1)} fusion(bf16[8192,768]{1,0:T(8,128)(2,1)S(1)} %copy-done, f32[128,8192]{1,0:T(8,128)} %get-tuple-element.65, f32[128]{0:T(128)S(1)} %get-tuple-element.25, s32[8192]{0:T(1024)S(1)} %iota_add_fusion, s32[128]{0:T(128)S(1)} %get-tuple-element.63, s32[128]{0:T(128)S(1)} %get-tuple-element.68), kind=kOutput, calls=%fused_computation.71 | convolution fusion | flops 1617002496 | bytes 17008128 | tf_op jit(solution)/shard_map/dot_general | solution.py:35
  42.3 0.0 collective-permute-done.1
  42.4 2.1 %collective-permute-start.8 = (bf16[128,768]{1,0:T(8,128)(2,1)S(1)}, bf16[128,768]{1,0:T(8,128)(2,1)S(1)}, u32[]{:S(2)}, u32[]{:S(2)}) collective-permute-start(bf16[128,768]{1,0:T(8,128)(2,1)S(1)} %copy-done.3), channel_id=1, source_target_pairs={{0,1},{1,2},{2,3},{3,4},{4,5},{5,6},{6,7},{7,8},{8,9},{9,10},{10,1... | collective-permute-start | bytes 589832 | tf_op jit(solution)/shard_map/ppermute | solution.py:16
  44.5 0.0 collective-permute-done.5
  44.5 0.0 collective-permute-done
  44.5 0.0 collective-permute-done.6
  44.5 0.0 collective-permute-done.3
  44.5 6.1 %convolution_multiply_fusion.2 = f32[128,8192]{1,0:T(8,128)} fusion(bf16[128,768]{1,0:T(8,128)(2,1)S(1)} %collective-permute-done.3, bf16[8192,768]{1,0:T(8,128)(2,1)S(1)} %copy-done), kind=kOutput, calls=%fused_computation.2 | convolution fusion | flops 1611661312 | bytes 16973824 | tf_op jit(solution)/shard_map/dot_general | solution.py:20
  50.6 2.9 %collective-permute-done.8 = bf16[128,768]{1,0:T(8,128)(2,1)S(1)} collective-permute-done((bf16[128,768]{1,0:T(8,128)(2,1)S(1)}, bf16[128,768]{1,0:T(8,128)(2,1)S(1)}, u32[]{:S(2)}, u32[]{:S(2)}) %collective-permute-start.8) | collective-permute-done | bytes 196640 | tf_op jit(solution)/shard_map/ppermute | solution.py:16
  53.6 14.8 %select_reduce_fusion.3 = (f32[128]{0:T(128)S(1)}, f32[128]{0:T(128)S(1)}, f32[128]{0:T(128)S(1)}, f32[128]{0:T(128)S(1)}, f32[128]{0:T(128)S(1)}, /*index=5*/f3...) fusion(f32[128,8192]{1,0:T(8,128)} %get-tuple-element.65, ...), kind=kOutput, calls=%fused_computation.6 | convolution fusion | flops 1655700096 | bytes 25408000 | tf_op jit(solution)/shard_map/dot_general | solution.py:20
  68.3 4.8 %fusion.69 = bf16[128,1,768]{2,0,1:T(8,128)(2,1)S(1)} fusion(bf16[8192,768]{1,0:T(8,128)(2,1)S(1)} %copy-done, f32[128,8192]{1,0:T(8,128)} %convolution_multiply_fusion.2, f32[128]{0:T(128)S(1)} %get-tuple-element.41, s32[8192]{0:T(1024)S(1)} %iota_add_fusion, s32[128]{0:T(128)S(1)} %get-tuple-element.72, s32[128]{0:T(128)S(1)} %get-tuple-element.70), kind=kOutput, calls=%fused_computation.74 | convolution fusion | flops 1617002496 | bytes 17008128 | tf_op jit(solution)/shard_map/dot_general | solution.py:35
  73.2 2.4 %fusion.66 = bf16[128,1,768]{2,0,1:T(8,128)(2,1)S(1)} fusion(bf16[8192,768]{1,0:T(8,128)(2,1)S(1)} %copy-done, f32[128,8192]{1,0:T(8,128)S(1)} %copy-done.1, f32[128]{0:T(128)S(1)} %get-tuple-element.40, s32[8192]{0:T(1024)S(1)} %iota_add_fusion, s32[128]{0:T(128)S(1)} %get-tuple-element.71, s32[128]{0:T(128)S(1)} %get-tuple-element.69), kind=kOutput, calls=%fused_computation.73 | convolution fusion | flops 1617002496 | bytes 17008128 | tf_op jit(solution)/shard_map/dot_general | solution.py:35
  75.7 2.4 %fusion.57 = bf16[128,1,768]{2,0,1:T(8,128)(2,1)S(1)} fusion(bf16[8192,768]{1,0:T(8,128)(2,1)S(1)} %copy-done, f32[128,8192]{1,0:T(8,128)S(1)} %copy-done.2, f32[128]{0:T(128)S(1)} %get-tuple-element.38, s32[8192]{0:T(1024)S(1)} %iota_add_fusion, s32[128]{0:T(128)S(1)} %get-tuple-element.59, s32[128]{0:T(128)S(1)} %get-tuple-element.57), kind=kOutput, calls=%fused_computation.70 | convolution fusion | flops 1617002496 | bytes 17008128 | tf_op jit(solution)/shard_map/dot_general | solution.py:35
  78.1 8.6 %select_reduce_fusion.5 = (f32[128]{0:T(128)S(1)}, f32[128]{0:T(128)S(1)}, f32[128]{0:T(128)S(1)}, f32[128]{0:T(128)S(1)}, f32[128]{0:T(128)S(1)}, /*index=5*/f3...) fusion(f32[128,8192]{1,0:T(8,128)S(1)} %copy-done.1, ...), kind=kLoop, calls=%fused_computation.8 | loop fusion | flops 37747456 | bytes 8432640 | tf_op jit(solution)/shard_map/reduce_sum | solution.py:39
  86.7 0.0 copy-start.4
  86.7 2.4 %fusion.54 = bf16[128,1,768]{2,0,1:T(8,128)(2,1)S(1)} fusion(bf16[8192,768]{1,0:T(8,128)(2,1)S(1)} %copy-done, f32[128,8192]{1,0:T(8,128)S(1)} %copy-done.2, f32[128]{0:T(128)S(1)} %get-tuple-element.37, s32[8192]{0:T(1024)S(1)} %iota_add_fusion, s32[128]{0:T(128)S(1)} %get-tuple-element.60, s32[128]{0:T(128)S(1)} %get-tuple-element.58), kind=kOutput, calls=%fused_computation.69 | convolution fusion | flops 1617002496 | bytes 17008128 | tf_op jit(solution)/shard_map/dot_general | solution.py:35
  89.2 1.9 %collective-permute-start.14 = (f32[128,2]{0,1:T(2,128)S(1)}, f32[128,2]{0,1:T(2,128)S(1)}, u32[]{:S(2)}, u32[]{:S(2)}) collective-permute-start(f32[128,2]{0,1:T(2,128)S(1)} %pad_maximum_fusion.9), channel_id=1, source_target_pairs={{0,1},{1,2},{2,3},{3,4},{4,5},{5,6},{6,7},{7,8},{8,9},{9,10},{10,1... | collective-permute-start | bytes 3080 | tf_op jit(solution)/shard_map/ppermute | solution.py:16
  91.1 7.9 %collective-permute-start.15 = (f32[128,2]{0,1:T(2,128)S(1)}, f32[128,2]{0,1:T(2,128)S(1)}, u32[]{:S(2)}, u32[]{:S(2)}) collective-permute-start(f32[128,2]{0,1:T(2,128)S(1)} %pad_maximum_fusion.10), channel_id=1, source_target_pairs={{1,0},{2,1},{3,2},{4,3},{5,4},{6,5},{7,6},{8,7},{9,8},{10,9},{11,1... | collective-permute-start | bytes 3080 | tf_op jit(solution)/shard_map/ppermute | solution.py:16
  99.0 1.9 %collective-permute-start.7 = (f32[128,2]{0,1:T(2,128)S(1)}, f32[128,2]{0,1:T(2,128)S(1)}, u32[]{:S(2)}, u32[]{:S(2)}) collective-permute-start(f32[128,2]{0,1:T(2,128)S(1)} %pad_maximum_fusion.5), channel_id=1, source_target_pairs={{1,0},{2,1},{3,2},{4,3},{5,4},{6,5},{7,6},{8,7},{9,8},{10,9},{11,1... | collective-permute-start | bytes 3080 | tf_op jit(solution)/shard_map/ppermute | solution.py:16
  101.0 1.9 %collective-permute-start.9 = (f32[128,2]{0,1:T(2,128)S(1)}, f32[128,2]{0,1:T(2,128)S(1)}, u32[]{:S(2)}, u32[]{:S(2)}) collective-permute-start(f32[128,2]{0,1:T(2,128)S(1)} %pad_maximum_fusion.6), channel_id=1, source_target_pairs={{1,0},{2,1},{3,2},{4,3},{5,4},{6,5},{7,6},{8,7},{9,8},{10,9},{11,1... | collective-permute-start | bytes 3080 | tf_op jit(solution)/shard_map/ppermute | solution.py:16
  102.9 3.9 %collective-permute-start.2 = (f32[128,2]{0,1:T(2,128)S(1)}, f32[128,2]{0,1:T(2,128)S(1)}, u32[]{:S(2)}, u32[]{:S(2)}) collective-permute-start(f32[128,2]{0,1:T(2,128)S(1)} %pad_maximum_fusion.2), channel_id=1, source_target_pairs={{0,1},{1,2},{2,3},{3,4},{4,5},{5,6},{6,7},{7,8},{8,9},{9,10},{10,1... | collective-permute-start | bytes 3080 | tf_op jit(solution)/shard_map/ppermute | solution.py:16
  107.0 0.0 collective-permute-done.14
  107.0 3.6 %collective-permute-start.4 = (f32[128,2]{0,1:T(2,128)S(1)}, f32[128,2]{0,1:T(2,128)S(1)}, u32[]{:S(2)}, u32[]{:S(2)}) collective-permute-start(f32[128,2]{0,1:T(2,128)S(1)} %pad_maximum_fusion.3), channel_id=1, source_target_pairs={{0,1},{1,2},{2,3},{3,4},{4,5},{5,6},{6,7},{7,8},{8,9},{9,10},{10,1... | collective-permute-start | bytes 3080 | tf_op jit(solution)/shard_map/ppermute | solution.py:16
  110.6 0.0 collective-permute-done.15
  110.6 1.9 %collective-permute-start.12 = (f32[128,2]{0,1:T(2,128)S(1)}, f32[128,2]{0,1:T(2,128)S(1)}, u32[]{:S(2)}, u32[]{:S(2)}) collective-permute-start(f32[128,2]{0,1:T(2,128)S(1)} %pad_maximum_fusion.7), channel_id=1, source_target_pairs={{0,1},{1,2},{2,3},{3,4},{4,5},{5,6},{6,7},{7,8},{8,9},{9,10},{10,1... | collective-permute-start | bytes 3080 | tf_op jit(solution)/shard_map/ppermute | solution.py:16
  112.6 0.0 collective-permute-done.7
  112.6 7.9 %collective-permute-start.13 = (f32[128,2]{0,1:T(2,128)S(1)}, f32[128,2]{0,1:T(2,128)S(1)}, u32[]{:S(2)}, u32[]{:S(2)}) collective-permute-start(f32[128,2]{0,1:T(2,128)S(1)} %pad_maximum_fusion.8), channel_id=1, source_target_pairs={{1,0},{2,1},{3,2},{4,3},{5,4},{6,5},{7,6},{8,7},{9,8},{10,9},{11,1... | collective-permute-start | bytes 3080 | tf_op jit(solution)/shard_map/ppermute | solution.py:16
  120.5 0.0 collective-permute-done.9
  120.5 1.9 %collective-permute-start.10 = (bf16[128,2,768]{2,0,1:T(8,128)(2,1)S(1)}, bf16[128,2,768]{2,0,1:T(8,128)(2,1)S(1)}, u32[]{:S(2)}, u32[]{:S(2)}) collective-permute-start(bf16[128,2,768]{2,0,1:T(8,128)(2,1)S(1)} %pad_maximum_fusion), channel_id=1, source_target_pairs={{0,1},{1,2},{2,3},{3,4},{4,5},{5,6},{6,7},{7,8},{8,9},{9,10},{10,1... | collective-permute-start | bytes 1179656 | tf_op jit(solution)/shard_map/ppermute | solution.py:16
  122.4 0.0 collective-permute-done.2
  122.4 7.9 %collective-permute-start.11 = (bf16[128,2,768]{2,0,1:T(8,128)(2,1)S(1)}, bf16[128,2,768]{2,0,1:T(8,128)(2,1)S(1)}, u32[]{:S(2)}, u32[]{:S(2)}) collective-permute-start(bf16[128,2,768]{2,0,1:T(8,128)(2,1)S(1)} %pad_maximum_fusion.1), channel_id=1, source_target_pairs={{1,0},{2,1},{3,2},{4,3},{5,4},{6,5},{7,6},{8,7},{9,8},{10,9},{11,1... | collective-permute-start | bytes 1179656 | tf_op jit(solution)/shard_map/ppermute | solution.py:16
  130.3 2.4 %fusion.63 = bf16[128,1,768]{2,0,1:T(8,128)(2,1)S(1)} fusion(bf16[8192,768]{1,0:T(8,128)(2,1)S(1)} %copy-done, f32[128,8192]{1,0:T(8,128)S(1)} %copy-done.4, f32[128]{0:T(128)S(1)} %get-tuple-element.24, s32[8192]{0:T(1024)S(1)} %iota_add_fusion, s32[128]{0:T(128)S(1)} %get-tuple-element.64, s32[128]{0:T(128)S(1)} %get-tuple-element.67), kind=kOutput, calls=%fused_computation.72 | convolution fusion | flops 1617002496 | bytes 17008128 | tf_op jit(solution)/shard_map/dot_general | solution.py:35
  132.7 0.0 collective-permute-done.4
  132.8 0.0 collective-permute-done.12
  132.8 0.0 collective-permute-done.13
  132.8 0.6 log_add_fusion
  133.4 0.4 collective-permute-done.10
  133.8 3.1 %collective-permute-done.11 = bf16[128,2,768]{2,0,1:T(8,128)(2,1)S(1)} collective-permute-done((bf16[128,2,768]{2,0,1:T(8,128)(2,1)S(1)}, bf16[128,2,768]{2,0,1:T(8,128)(2,1)S(1)}, u32[]{:S(2)}, u32[]{:S(2)}) %collective-permute-start.11) | collective-permute-done | bytes 393248 | tf_op jit(solution)/shard_map/ppermute | solution.py:16
  136.8 0.3 divide_convert_fusion
  137.2 1.2 copy.7
  (21 shorter events, 0.2 us)
Async XLA Ops:
  0.6 43.8 %collective-permute-start.5 = (s32[128,2]{0,1:T(2,128)}, s32[128,2]{0,1:T(2,128)S(1)}, u32[]{:S(2)}, u32[]{:S(2)}) collective-permute-start(s32[128,2]{0,1:T(2,128)} %param.6), channel_id=1, source_target_pairs={{0,1},{1,2},{2,3},{3,4},{4,5},{5,6},{6,7},{7,8},{8,9},{9,10},{10,1... | collective-permute-start | bytes 3080 | tf_op jit(solution)/shard_map/ppermute | solution.py:16
  3.7 40.8 %collective-permute-start = (s32[128,2]{0,1:T(2,128)}, s32[128,2]{0,1:T(2,128)S(1)}, u32[]{:S(2)}, u32[]{:S(2)}) collective-permute-start(s32[128,2]{0,1:T(2,128)} %param.6), channel_id=1, source_target_pairs={{1,0},{2,1},{3,2},{4,3},{5,4},{6,5},{7,6},{8,7},{9,8},{10,9},{11,1... | collective-permute-start | bytes 3080 | tf_op jit(solution)/shard_map/ppermute | solution.py:16
  12.2 30.1 %collective-permute-start.1 = (s32[128,2]{0,1:T(2,128)}, s32[128,2]{0,1:T(2,128)S(1)}, u32[]{:S(2)}, u32[]{:S(2)}) collective-permute-start(s32[128,2]{0,1:T(2,128)} %param.7), channel_id=1, source_target_pairs={{1,0},{2,1},{3,2},{4,3},{5,4},{6,5},{7,6},{8,7},{9,8},{10,9},{11,1... | collective-permute-start | bytes 3080 | tf_op jit(solution)/shard_map/ppermute | solution.py:16
  15.6 28.9 %collective-permute-start.6 = (s32[128,2]{0,1:T(2,128)}, s32[128,2]{0,1:T(2,128)S(1)}, u32[]{:S(2)}, u32[]{:S(2)}) collective-permute-start(s32[128,2]{0,1:T(2,128)} %param.7), channel_id=1, source_target_pairs={{0,1},{1,2},{2,3},{3,4},{4,5},{5,6},{6,7},{7,8},{8,9},{9,10},{10,1... | collective-permute-start | bytes 3080 | tf_op jit(solution)/shard_map/ppermute | solution.py:16
  18.0 26.5 %collective-permute-start.3 = (bf16[128,768]{1,0:T(8,128)(2,1)}, bf16[128,768]{1,0:T(8,128)(2,1)S(1)}, u32[]{:S(2)}, u32[]{:S(2)}) collective-permute-start(bf16[128,768]{1,0:T(8,128)(2,1)} %param.4), channel_id=1, source_target_pairs={{1,0},{2,1},{3,2},{4,3},{5,4},{6,5},{7,6},{8,7},{9,8},{10,9},{11,1... | collective-permute-start | bytes 589832 | tf_op jit(solution)/shard_map/ppermute | solution.py:16
  26.1 11.7 %copy-start = (bf16[8192,768]{1,0:T(8,128)(2,1)S(1)}, bf16[8192,768]{1,0:T(8,128)(2,1)}, u32[]{:S(2)}) copy-start(bf16[8192,768]{1,0:T(8,128)(2,1)} %param.5) | copy-start | bytes 37748740
  37.8 4.5 %copy-start.3 = (bf16[128,768]{1,0:T(8,128)(2,1)S(1)}, bf16[128,768]{1,0:T(8,128)(2,1)}, u32[]{:S(2)}) copy-start(bf16[128,768]{1,0:T(8,128)(2,1)} %param.4) | copy-start | bytes 589828
  42.4 11.2 %collective-permute-start.8 = (bf16[128,768]{1,0:T(8,128)(2,1)S(1)}, bf16[128,768]{1,0:T(8,128)(2,1)S(1)}, u32[]{:S(2)}, u32[]{:S(2)}) collective-permute-start(bf16[128,768]{1,0:T(8,128)(2,1)S(1)} %copy-done.3), channel_id=1, source_target_pairs={{0,1},{1,2},{2,3},{3,4},{4,5},{5,6},{6,7},{7,8},{8,9},{9,10},{10,1... | collective-permute-start | bytes 589832 | tf_op jit(solution)/shard_map/ppermute | solution.py:16
  68.3 4.9 %copy-start.1 = (f32[128,8192]{1,0:T(8,128)S(1)}, f32[128,8192]{1,0:T(8,128)}, u32[]{:S(2)}) copy-start(f32[128,8192]{1,0:T(8,128)} %convolution_multiply_fusion.2) | copy-start | bytes 12582916
  73.2 2.5 %copy-start.2 = (f32[128,8192]{1,0:T(8,128)S(1)}, f32[128,8192]{1,0:T(8,128)}, u32[]{:S(2)}) copy-start(f32[128,8192]{1,0:T(8,128)} %get-tuple-element.66) | copy-start | bytes 12582916
  86.7 43.6 %copy-start.4 = (f32[128,8192]{1,0:T(8,128)S(1)}, f32[128,8192]{1,0:T(8,128)}, u32[]{:S(2)}) copy-start(f32[128,8192]{1,0:T(8,128)} %get-tuple-element.65) | copy-start | bytes 12582916
  89.2 17.8 %collective-permute-start.14 = (f32[128,2]{0,1:T(2,128)S(1)}, f32[128,2]{0,1:T(2,128)S(1)}, u32[]{:S(2)}, u32[]{:S(2)}) collective-permute-start(f32[128,2]{0,1:T(2,128)S(1)} %pad_maximum_fusion.9), channel_id=1, source_target_pairs={{0,1},{1,2},{2,3},{3,4},{4,5},{5,6},{6,7},{7,8},{8,9},{9,10},{10,1... | collective-permute-start | bytes 3080 | tf_op jit(solution)/shard_map/ppermute | solution.py:16
  91.1 19.5 %collective-permute-start.15 = (f32[128,2]{0,1:T(2,128)S(1)}, f32[128,2]{0,1:T(2,128)S(1)}, u32[]{:S(2)}, u32[]{:S(2)}) collective-permute-start(f32[128,2]{0,1:T(2,128)S(1)} %pad_maximum_fusion.10), channel_id=1, source_target_pairs={{1,0},{2,1},{3,2},{4,3},{5,4},{6,5},{7,6},{8,7},{9,8},{10,9},{11,1... | collective-permute-start | bytes 3080 | tf_op jit(solution)/shard_map/ppermute | solution.py:16
  99.0 13.6 %collective-permute-start.7 = (f32[128,2]{0,1:T(2,128)S(1)}, f32[128,2]{0,1:T(2,128)S(1)}, u32[]{:S(2)}, u32[]{:S(2)}) collective-permute-start(f32[128,2]{0,1:T(2,128)S(1)} %pad_maximum_fusion.5), channel_id=1, source_target_pairs={{1,0},{2,1},{3,2},{4,3},{5,4},{6,5},{7,6},{8,7},{9,8},{10,9},{11,1... | collective-permute-start | bytes 3080 | tf_op jit(solution)/shard_map/ppermute | solution.py:16
  101.0 19.5 %collective-permute-start.9 = (f32[128,2]{0,1:T(2,128)S(1)}, f32[128,2]{0,1:T(2,128)S(1)}, u32[]{:S(2)}, u32[]{:S(2)}) collective-permute-start(f32[128,2]{0,1:T(2,128)S(1)} %pad_maximum_fusion.6), channel_id=1, source_target_pairs={{1,0},{2,1},{3,2},{4,3},{5,4},{6,5},{7,6},{8,7},{9,8},{10,9},{11,1... | collective-permute-start | bytes 3080 | tf_op jit(solution)/shard_map/ppermute | solution.py:16
  102.9 19.5 %collective-permute-start.2 = (f32[128,2]{0,1:T(2,128)S(1)}, f32[128,2]{0,1:T(2,128)S(1)}, u32[]{:S(2)}, u32[]{:S(2)}) collective-permute-start(f32[128,2]{0,1:T(2,128)S(1)} %pad_maximum_fusion.2), channel_id=1, source_target_pairs={{0,1},{1,2},{2,3},{3,4},{4,5},{5,6},{6,7},{7,8},{8,9},{9,10},{10,1... | collective-permute-start | bytes 3080 | tf_op jit(solution)/shard_map/ppermute | solution.py:16
  107.0 25.8 %collective-permute-start.4 = (f32[128,2]{0,1:T(2,128)S(1)}, f32[128,2]{0,1:T(2,128)S(1)}, u32[]{:S(2)}, u32[]{:S(2)}) collective-permute-start(f32[128,2]{0,1:T(2,128)S(1)} %pad_maximum_fusion.3), channel_id=1, source_target_pairs={{0,1},{1,2},{2,3},{3,4},{4,5},{5,6},{6,7},{7,8},{8,9},{9,10},{10,1... | collective-permute-start | bytes 3080 | tf_op jit(solution)/shard_map/ppermute | solution.py:16
  110.6 22.1 %collective-permute-start.12 = (f32[128,2]{0,1:T(2,128)S(1)}, f32[128,2]{0,1:T(2,128)S(1)}, u32[]{:S(2)}, u32[]{:S(2)}) collective-permute-start(f32[128,2]{0,1:T(2,128)S(1)} %pad_maximum_fusion.7), channel_id=1, source_target_pairs={{0,1},{1,2},{2,3},{3,4},{4,5},{5,6},{6,7},{7,8},{8,9},{9,10},{10,1... | collective-permute-start | bytes 3080 | tf_op jit(solution)/shard_map/ppermute | solution.py:16
  112.6 20.2 %collective-permute-start.13 = (f32[128,2]{0,1:T(2,128)S(1)}, f32[128,2]{0,1:T(2,128)S(1)}, u32[]{:S(2)}, u32[]{:S(2)}) collective-permute-start(f32[128,2]{0,1:T(2,128)S(1)} %pad_maximum_fusion.8), channel_id=1, source_target_pairs={{1,0},{2,1},{3,2},{4,3},{5,4},{6,5},{7,6},{8,7},{9,8},{10,9},{11,1... | collective-permute-start | bytes 3080 | tf_op jit(solution)/shard_map/ppermute | solution.py:16
  120.5 13.3 %collective-permute-start.10 = (bf16[128,2,768]{2,0,1:T(8,128)(2,1)S(1)}, bf16[128,2,768]{2,0,1:T(8,128)(2,1)S(1)}, u32[]{:S(2)}, u32[]{:S(2)}) collective-permute-start(bf16[128,2,768]{2,0,1:T(8,128)(2,1)S(1)} %pad_maximum_fusion), channel_id=1, source_target_pairs={{0,1},{1,2},{2,3},{3,4},{4,5},{5,6},{6,7},{7,8},{8,9},{9,10},{10,1... | collective-permute-start | bytes 1179656 | tf_op jit(solution)/shard_map/ppermute | solution.py:16
  122.4 14.4 %collective-permute-start.11 = (bf16[128,2,768]{2,0,1:T(8,128)(2,1)S(1)}, bf16[128,2,768]{2,0,1:T(8,128)(2,1)S(1)}, u32[]{:S(2)}, u32[]{:S(2)}) collective-permute-start(bf16[128,2,768]{2,0,1:T(8,128)(2,1)S(1)} %pad_maximum_fusion.1), channel_id=1, source_target_pairs={{1,0},{2,1},{3,2},{4,3},{5,4},{6,5},{7,6},{8,7},{9,8},{10,9},{11,1... | collective-permute-start | bytes 1179656 | tf_op jit(solution)/shard_map/ppermute | solution.py:16
where the time goes:
time: 139 us; the launch traced here: 138 us
  starting transfers between devices  67.5 us (49%)
  matrix products  51.7 us (37%)
  other arithmetic  9.66 us (7%)
  waiting for transfers between devices  6.42 us (5%)
  local copies, waits for them, and re-layouts  1.95 us (1%)
    ppermute x16, starting transfers between devices, shifted(): return lax.ppermute(shard, axis, pairs)  67.5 us
    dot_general x3, matrix products, block_state(): lax.dot_general(query_rows, block, (((1,), (1,)), ((), ())), preferred_el...  32.5 us
    dot_general x6, matrix products, block_state(): jnp.dot(weights.astype(jnp.bfloat16), block, preferred_element_type=jnp.f...  19.2 us
    reduce_sum x1, other arithmetic, block_state(): score_sums.append(jnp.sum(jnp.where(inside, scores, 0.0), axis=1))  8.58 us
    ppermute x16, waiting for transfers between devices, shifted(): return lax.ppermute(shard, axis, pairs)  6.42 us
  transfers between devices with their start and end apart: 16, of which 3 were waited for; matrix products, arithmetic and copies ran while one was open for 19% of the time, Pallas kernels for 0%

commit v1 on v0

v1 whole, which is shorter than its diff:
```python
import functools
import math

import jax
import jax.numpy as jnp
from jax import lax
from jax.experimental import pallas as pl
from jax.experimental.pallas import tpu as pltpu
from jax.sharding import PartitionSpec as P

NEG_FILL = -1e30
SCORE_SCALE = 3.0
LOG2E = math.log2(math.e)
LN2 = math.log(2.0)
MESH = pl.DeviceIdType.MESH

CHUNK = 1024


def fold_rows(op, x):
    rows, cols = x.shape
    return op(x.reshape(rows // 8, 8, cols), axis=0)


def kernel(
    n_dev,
    n_pb,
    scale,
    q_hbm,
    c_hbm,
    start_hbm,
    stop_hbm,
    pooled_ref,
    log_mass_ref,
    mean_ref,
    c_v,
    c_t,
    xm,
    q_v,
    q_in,
    q_t,
    w_v,
    w_in,
    maxs,
    sums,
    tots,
    acc,
    acc_own,
    parts_out,
    parts_in,
    stats_out,
    stats_in,
    c_sem,
    local_sem,
    q_send,
    q_recv,
    w_send,
    w_recv,
    p_send,
    p_recv,
    s_send,
    s_recv,
):
    n_q, dim = q_hbm.shape
    n_doc = c_hbm.shape[0]
    chunks = n_doc // CHUNK
    me = lax.axis_index("tm") * n_pb + lax.axis_index("pb")

    def coords(pos):
        return (pos // n_pb, pos % n_pb)

    prior = coords((me + n_dev - 1) % n_dev)
    following = coords((me + 1) % n_dev)

    def c_copy(i):
        rows = pl.ds(pl.multiple_of(i * CHUNK, CHUNK), CHUNK)
        return pltpu.make_async_copy(c_hbm.at[rows, :], c_v.at[rows, :], c_sem.at[i])

    q_copy = pltpu.make_async_copy(q_hbm, q_v, local_sem.at[0])
    start_copy = pltpu.make_async_copy(start_hbm, w_v.at[0], local_sem.at[1])
    stop_copy = pltpu.make_async_copy(stop_hbm, w_v.at[1], local_sem.at[2])
    q_copy.start()
    start_copy.start()
    stop_copy.start()
    lax.fori_loop(0, chunks, lambda i, _: (c_copy(i).start(), 0)[1], 0)

    barrier = pltpu.get_barrier_semaphore()
    for neighbour in (prior, following):
        pl.semaphore_signal(barrier, inc=1, device_id=neighbour, device_id_type=MESH)
    pl.semaphore_wait(barrier, 2)
    q_copy.wait()
    start_copy.wait()
    stop_copy.wait()

    out_copies, q_copies, p_copies, s_copies = [], {}, {}, {}
    for slot, neighbour in ((1, prior), (0, following)):
        for src, dst, send, recv in (
            (w_v, w_in, w_send, w_recv),
            (q_v, q_in, q_send, q_recv),
        ):
            copy = pltpu.make_async_remote_copy(
                src_ref=src,
                dst_ref=dst.at[slot],
                send_sem=send.at[slot],
                recv_sem=recv.at[slot],
                device_id=neighbour,
                device_id_type=MESH,
            )
            copy.start()
            out_copies.append(copy)
            q_copies.setdefault(slot, []).append(copy)

    start_doc = me * n_doc

    def scores_pass(rhs, bounds, targets, base, cols, transpose):
        width = rhs.shape[1]
        for w in range(2):
            maxs[base + w, :, :width] = jnp.full((8, width), NEG_FILL, jnp.float32)
            sums[base + w, :, :width] = jnp.zeros((8, width), jnp.float32)

        def body(i, carry):
            rows = pl.ds(pl.multiple_of(i * CHUNK, CHUNK), CHUNK)
            if transpose:
                c_copy(i).wait()
            block = c_v[rows, :]
            x = jnp.dot(block, rhs[...], preferred_element_type=jnp.float32) * (scale * LOG2E)
            if transpose:
                c_t[:, rows] = block.T
            doc = lax.broadcasted_iota(jnp.int32, (CHUNK, width), 0)
            for w in range(2):
                low, size = bounds[w]
                offset = (i * CHUNK - low).astype(jnp.int32)
                inside = (doc + offset).astype(jnp.uint32) < size.astype(jnp.uint32)
                kept = jnp.where(inside, x, NEG_FILL)
                xm[targets[w], rows, cols[w]] = kept
                maxs[base + w, :, :width] = jnp.maximum(
                    maxs[base + w, :, :width], fold_rows(jnp.max, kept)
                )
                sums[base + w, :, :width] += fold_rows(jnp.sum, jnp.where(inside, x, 0.0))
            return carry

        lax.fori_loop(0, chunks, body, 0)

    def parts_pass(source, top, out):
        out[...] = jnp.zeros_like(out)
        tots[...] = jnp.zeros_like(tots)

        def body(i, carry):
            rows = pl.ds(pl.multiple_of(i * CHUNK, CHUNK), CHUNK)
            weights = jnp.exp2(xm[source, rows, :] - top)
            tots[...] += fold_rows(jnp.sum, weights)
            out[...] += jnp.dot(
                c_t[:, rows], weights.astype(jnp.bfloat16), preferred_element_type=jnp.float32
            )
            return carry

        lax.fori_loop(0, chunks, body, 0)
        return jnp.sum(tots[...], axis=0, keepdims=True)

    q_t[:, pl.ds(0, n_q)] = q_v[...].T
    own_bounds = []
    for w in range(2):
        low = w_v[0, w : w + 1, :]
        own_bounds.append((low - start_doc, w_v[1, w : w + 1, :] - low))
    scores_pass(
        q_t.at[:, pl.ds(0, n_q)],
        own_bounds,
        (0, 0),
        0,
        (pl.ds(0, n_q), pl.ds(n_q, n_q)),
        True,
    )
    own_top = [jnp.max(maxs[w, :, :n_q], axis=0, keepdims=True) for w in range(2)]
    own_sum = [jnp.sum(sums[w, :, :n_q], axis=0, keepdims=True) for w in range(2)]
    own_tot = parts_pass(0, jnp.concatenate(own_top, axis=1), acc_own)

    for slot in range(2):
        for copy in q_copies[slot]:
            copy.wait_recv()
    for slot in range(2):
        q_t[:, pl.ds(slot * n_q, n_q)] = q_in[slot].T
    bounds = []
    for w in range(2):
        low = jnp.concatenate([w_in[slot, 0, w : w + 1, :] for slot in range(2)], axis=1)
        stop = jnp.concatenate([w_in[slot, 1, w : w + 1, :] for slot in range(2)], axis=1)
        bounds.append((low - start_doc, stop - low))
    scores_pass(q_t, bounds, (0, 1), 0, (pl.ds(0, 2 * n_q),) * 2, False)
    back = (prior, following)
    for w in range(2):
        top = jnp.max(maxs[w], axis=0, keepdims=True)
        total = jnp.sum(sums[w], axis=0, keepdims=True)
        mass = parts_pass(w, top, acc)
        for slot in range(2):
            half = slice(slot * n_q, (slot + 1) * n_q)
            stats_out[slot, 3 * w : 3 * w + 1, :] = top[:, half]
            stats_out[slot, 3 * w + 1 : 3 * w + 2, :] = mass[:, half]
            stats_out[slot, 3 * w + 2 : 3 * w + 3, :] = total[:, half]
            parts_out[slot, w] = acc[:, half].astype(jnp.bfloat16)
        for slot in range(2):
            copy = pltpu.make_async_remote_copy(
                src_ref=parts_out.at[slot, w],
                dst_ref=parts_in.at[1 - slot, w],
                send_sem=p_send.at[slot, w],
                recv_sem=p_recv.at[1 - slot, w],
                device_id=back[slot],
                device_id_type=MESH,
            )
            copy.start()
            out_copies.append(copy)
            p_copies[1 - slot, w] = copy
    for slot in range(2):
        copy = pltpu.make_async_remote_copy(
            src_ref=stats_out.at[slot],
            dst_ref=stats_in.at[1 - slot],
            send_sem=s_send.at[slot],
            recv_sem=s_recv.at[1 - slot],
            device_id=back[slot],
            device_id_type=MESH,
        )
        copy.start()
        out_copies.append(copy)
        s_copies[1 - slot] = copy

    for slot in range(2):
        s_copies[slot].wait_recv()
    for w in range(2):
        half = slice(w * n_q, (w + 1) * n_q)
        tops = [own_top[w]] + [stats_in[slot, 3 * w : 3 * w + 1, :] for slot in range(2)]
        masses = [own_tot[:, half]] + [
            stats_in[slot, 3 * w + 1 : 3 * w + 2, :] for slot in range(2)
        ]
        totals = [own_sum[w]] + [stats_in[slot, 3 * w + 2 : 3 * w + 3, :] for slot in range(2)]
        best = jnp.maximum(jnp.maximum(tops[0], tops[1]), tops[2])
        factors = [jnp.exp2(top - best) for top in tops]
        mass = sum(f * m for f, m in zip(factors, masses))
        log_mass_ref[w : w + 1, :] = best * LN2 + jnp.log(mass)
        size = own_bounds[w][1].astype(jnp.float32)
        mean_ref[w : w + 1, :] = (totals[0] + totals[1] + totals[2]) * LN2 / size
        shares = [f / mass for f in factors]
        for slot in range(2):
            p_copies[slot, w].wait_recv()
        pooled = acc_own[:, half] * shares[0]
        for slot in range(2):
            pooled += parts_in[slot, w].astype(jnp.float32) * shares[1 + slot]
        pooled_ref[:, pl.ds(w * dim, dim)] = pooled.astype(jnp.bfloat16).T

    for copy in out_copies:
        copy.wait_send()


def solution(mesh):
    n_dev = mesh.shape["tm"] * mesh.shape["pb"]
    n_pb = mesh.shape["pb"]

    def local(queries, corpus, window_start, window_end):
        n_q, dim = queries.shape
        n_doc = corpus.shape[0]
        chunks = n_doc // CHUNK
        scale = SCORE_SCALE / math.sqrt(dim)
        any_spec = pl.BlockSpec(memory_space=pl.ANY)
        vmem_spec = pl.BlockSpec(memory_space=pltpu.VMEM)
        dma = pltpu.SemaphoreType.DMA
        pooled, log_mass, mean_score = pl.pallas_call(
            functools.partial(kernel, n_dev, n_pb, scale),
            out_shape=(
                jax.ShapeDtypeStruct((n_q, 2 * dim), jnp.bfloat16),
                jax.ShapeDtypeStruct((2, n_q), jnp.float32),
                jax.ShapeDtypeStruct((2, n_q), jnp.float32),
            ),
            in_specs=[any_spec] * 4,
            out_specs=(vmem_spec,) * 3,
            scratch_shapes=[
                pltpu.VMEM((n_doc, dim), jnp.bfloat16),
                pltpu.VMEM((dim, n_doc), jnp.bfloat16),
                pltpu.VMEM((2, n_doc, 2 * n_q), jnp.float32),
                pltpu.VMEM((n_q, dim), jnp.bfloat16),
                pltpu.VMEM((2, n_q, dim), jnp.bfloat16),
                pltpu.VMEM((dim, 2 * n_q), jnp.bfloat16),
                pltpu.VMEM((2, 2, n_q), jnp.int32),
                pltpu.VMEM((2, 2, 2, n_q), jnp.int32),
                pltpu.VMEM((2, 8, 2 * n_q), jnp.float32),
                pltpu.VMEM((2, 8, 2 * n_q), jnp.float32),
                pltpu.VMEM((8, 2 * n_q), jnp.float32),
                pltpu.VMEM((dim, 2 * n_q), jnp.float32),
                pltpu.VMEM((dim, 2 * n_q), jnp.float32),
                pltpu.VMEM((2, 2, dim, n_q), jnp.bfloat16),
                pltpu.VMEM((2, 2, dim, n_q), jnp.bfloat16),
                pltpu.VMEM((2, 8, n_q), jnp.float32),
                pltpu.VMEM((2, 8, n_q), jnp.float32),
                dma((chunks,)),
                dma((3,)),
                dma((2,)),
                dma((2,)),
                dma((2,)),
                dma((2,)),
                dma((2, 2)),
                dma((2, 2)),
                dma((2,)),
                dma((2,)),
            ],
            compiler_params=pltpu.CompilerParams(
                collective_id=0,
                has_side_effects=True,
                vmem_limit_bytes=60 * 1024 * 1024,
            ),
            name="window_pool",
        )(queries, corpus, window_start.T, window_end.T)
        return pooled.reshape(n_q, 2, dim), log_mass.T, mean_score.T

    rows = P(("tm", "pb"), None)
    return jax.shard_map(
        local,
        mesh=mesh,
        in_specs=(rows,) * 4,
        out_specs=(P(("tm", "pb"), None, None), rows, rows),
        check_vma=False,
    )
```

time: 139 us -> 52 us (0.37)
  the two profiles are of different devices: /device:TPU:4 before, /device:TPU:1 now
where the time goes in v1:
time: 52 us; the launch traced here: 51.9 us
  Pallas kernels  47 us (90%)
  local copies, waits for them, and re-layouts  4.27 us (8%)
  between operations  0.64 us (1%)
    pallas_call x1, Pallas kernels, local(): pl.pallas_call(functools.partial(kernel, n_dev, n_pb, scale), out_shape=(...  47 us
    unnamed x2, local copies, waits for them, and re-layouts  2.44 us
    reshape x1, local copies, waits for them, and re-layouts, local(): return (pooled.reshape(n_q, 2, dim), log_mass.T, mean_score.T)  1.83 us

profile of v1, /device:TPU:1, one launch (start us, length us, event | category | flops | bytes accessed | tf_op | source)
XLA Modules:
  0.0 51.9 jit_solution(8610596945381642348)
XLA Ops:
  0.6 47.0 %window_pool.1 = (bf16[128,1536]{1,0:T(8,128)(2,1)}, f32[2,128]{1,0:T(2,128)}, f32[2,128]{1,0:T(2,128)}) custom-call(bf16[128,768]{1,0:T(8,128)(2,1)} %q_hbm.1, bf16[8192,768]{1,0:T(8,128)(2,1)} %c_hbm.1, s32[2,128]{1,0:T(2,128)} %bitcast.6, s32[2,128]{1,0:T(2,128)} %bitcast.7), custom_call_target="tpu_custom_call" | custom-call | tf_op jit(solution)/shard_map/window_pool/pallas_call | solution.py:263
  47.6 1.8 %reshape.9 = bf16[128,2,768]{2,1,0:T(2,128)(2,1)} reshape(bf16[128,1536]{1,0:T(8,128)(2,1)} %get-tuple-element.6) | data formatting | bytes 786432 | tf_op jit(solution)/shard_map/reshape | solution.py:308
  49.4 1.2 %copy.9 = f32[128,2]{0,1:T(2,128)} copy(f32[128,2]{0,1:T(2,128)} %bitcast.5) | data formatting | bytes 2048
  50.6 1.2 %copy.10 = f32[128,2]{0,1:T(2,128)} copy(f32[128,2]{0,1:T(2,128)} %bitcast.4) | data formatting | bytes 2048

commit v2 on v1

v2 whole, which is shorter than its diff:
```python
import functools
import math

import jax
import jax.numpy as jnp
from jax import lax
from jax.experimental import pallas as pl
from jax.experimental.pallas import tpu as pltpu
from jax.sharding import PartitionSpec as P

NEG_FILL = -1e30
SCORE_SCALE = 3.0
LOG2E = math.log2(math.e)
MESH = pl.DeviceIdType.MESH

COPY_ROWS = 1024
OWN_ROWS = 2048
ROWS = 2048
PART_ROWS = 2048


def fold_rows(op, x):
    rows, cols = x.shape
    return op(x.reshape(rows // 8, 8, cols), axis=0)


def kernel(
    n_dev,
    n_pb,
    scale,
    q_hbm,
    c_hbm,
    start_hbm,
    stop_hbm,
    pooled_ref,
    best_ref,
    log_ref,
    total_ref,
    size_ref,
    c_v,
    c_t,
    xm,
    q_v,
    q_in,
    q_t,
    w_v,
    w_in,
    maxs,
    sums,
    tots,
    acc,
    acc_own,
    swap_out,
    swap_in,
    comb_out,
    comb_in,
    swap_stat_out,
    swap_stat_in,
    comb_stat_out,
    comb_stat_in,
    c_sem,
    local_sem,
    q_send,
    q_recv,
    w_send,
    w_recv,
    swap_send,
    swap_recv,
    comb_send,
    comb_recv,
):
    n_q, dim = q_hbm.shape
    n_doc = c_hbm.shape[0]
    me = lax.axis_index("tm") * n_pb + lax.axis_index("pb")

    def device(step):
        pos = (me + n_dev + step) % n_dev
        return (pos // n_pb, pos % n_pb)

    def send(src, dst, send_sem, recv_sem, step):
        return pltpu.make_async_remote_copy(
            src_ref=src,
            dst_ref=dst,
            send_sem=send_sem,
            recv_sem=recv_sem,
            device_id=device(step),
            device_id_type=MESH,
        )

    def c_copy(i):
        rows = pl.ds(pl.multiple_of(i * COPY_ROWS, COPY_ROWS), COPY_ROWS)
        return pltpu.make_async_copy(c_hbm.at[rows, :], c_v.at[rows, :], c_sem.at[i])

    q_copy = pltpu.make_async_copy(q_hbm, q_v, local_sem.at[0])
    start_copy = pltpu.make_async_copy(start_hbm, w_v.at[0], local_sem.at[1])
    stop_copy = pltpu.make_async_copy(stop_hbm, w_v.at[1], local_sem.at[2])
    q_copy.start()
    start_copy.start()
    stop_copy.start()
    lax.fori_loop(0, n_doc // COPY_ROWS, lambda i, _: (c_copy(i).start(), 0)[1], 0)

    barrier = pltpu.get_barrier_semaphore()
    for step in (-2, -1, 1, 2):
        pl.semaphore_signal(barrier, inc=1, device_id=device(step), device_id_type=MESH)
    pl.semaphore_wait(barrier, 4)
    q_copy.wait()
    start_copy.wait()
    stop_copy.wait()

    q_copies = []
    for slot, step in ((1, -1), (0, 1)):
        q_copies.append(send(w_v, w_in.at[slot], w_send.at[slot], w_recv.at[slot], step))
        q_copies.append(send(q_v, q_in.at[slot], q_send.at[slot], q_recv.at[slot], step))
    for copy in q_copies:
        copy.start()

    start_doc = me * n_doc

    def scores_pass(rhs, bounds, targets, cols, step_rows, first):
        width = rhs.shape[1]
        for w in range(2):
            maxs[w, :, :width] = jnp.full((8, width), NEG_FILL, jnp.float32)

        def body(i, carry):
            rows = pl.ds(pl.multiple_of(i * step_rows, step_rows), step_rows)
            if first:
                for part in range(step_rows // COPY_ROWS):
                    c_copy(i * (step_rows // COPY_ROWS) + part).wait()
            block = c_v[rows, :]
            x = jnp.dot(block, rhs[...], preferred_element_type=jnp.float32)
            if first:
                c_t[:, rows] = block.T
            doc = lax.broadcasted_iota(jnp.int32, (step_rows, width), 0)
            for w in range(2):
                low, size = bounds[w]
                offset = i * step_rows - low
                inside = (doc + offset).astype(jnp.uint32) < size.astype(jnp.uint32)
                kept = jnp.where(inside, x, NEG_FILL)
                xm[targets[w], rows, cols[w]] = kept
                maxs[w, :, :width] = jnp.maximum(maxs[w, :, :width], fold_rows(jnp.max, kept))
            return carry

        lax.fori_loop(0, n_doc // step_rows, body, 0)
        return [jnp.max(maxs[w, :, :width], axis=0, keepdims=True) for w in range(2)]

    def parts_pass(source, top, out, part, of):
        chunks = n_doc // PART_ROWS
        if part == 0:
            out[...] = jnp.zeros_like(out)
            tots[...] = jnp.zeros_like(tots)
            sums[...] = jnp.zeros_like(sums)

        def body(i, carry):
            rows = pl.ds(pl.multiple_of(i * PART_ROWS, PART_ROWS), PART_ROWS)
            kept = xm[source, rows, :]
            weights = jnp.exp2((kept - top) * (scale * LOG2E))
            tots[...] += fold_rows(jnp.sum, weights)
            sums[...] += fold_rows(jnp.sum, jnp.where(kept > 0.5 * NEG_FILL, kept, 0.0))
            low = weights.astype(jnp.bfloat16)
            for half in range(2):
                span = pl.ds(half * (dim // 2), dim // 2)
                out[span, :] += jnp.dot(c_t[span, rows], low, preferred_element_type=jnp.float32)
            return carry

        lax.fori_loop(part * chunks // of, (part + 1) * chunks // of, body, 0)
        return (
            jnp.sum(tots[...], axis=0, keepdims=True),
            jnp.sum(sums[...], axis=0, keepdims=True),
        )

    def halves(x):
        return x[:, :n_q], x[:, n_q:]

    q_t[:, pl.ds(0, n_q)] = q_v[...].T
    own_bounds = []
    for w in range(2):
        low = w_v[0, w : w + 1, :]
        own_bounds.append((low - start_doc, w_v[1, w : w + 1, :] - low))
    own_top = scores_pass(
        q_t.at[:, pl.ds(0, n_q)],
        own_bounds,
        (0, 0),
        (pl.ds(0, n_q), pl.ds(n_q, n_q)),
        OWN_ROWS,
        True,
    )
    own_tot, own_sum = map(
        halves, parts_pass(0, jnp.concatenate(own_top, axis=1), acc_own, 0, 1)
    )

    for copy in q_copies:
        copy.wait_recv()
    for slot in range(2):
        q_t[:, pl.ds(slot * n_q, n_q)] = q_in[slot].T
    bounds = []
    for w in range(2):
        low = jnp.concatenate([w_in[slot, 0, w : w + 1, :] for slot in range(2)], axis=1)
        stop = jnp.concatenate([w_in[slot, 1, w : w + 1, :] for slot in range(2)], axis=1)
        bounds.append((low - start_doc, stop - low))
    tops = scores_pass(q_t, bounds, (0, 1), (pl.ds(0, 2 * n_q),) * 2, ROWS, False)

    swaps, combs = [], []
    for w in range(2):
        swap_step, comb_step = ((-2, 1), (2, -1))[w]
        sem = (swap_send, swap_recv)
        swaps.append(
            [
                send(swap_out.at[w], swap_in.at[w], sem[0].at[w, 0], sem[1].at[w, 0], swap_step),
                send(
                    swap_stat_out.at[w],
                    swap_stat_in.at[w],
                    sem[0].at[w, 1],
                    sem[1].at[w, 1],
                    swap_step,
                ),
            ]
        )
        sem = (comb_send, comb_recv)
        combs.append(
            [
                send(comb_out.at[w], comb_in.at[w], sem[0].at[w, 0], sem[1].at[w, 0], comb_step),
                send(
                    comb_stat_out.at[w],
                    comb_stat_in.at[w],
                    sem[0].at[w, 1],
                    sem[1].at[w, 1],
                    comb_step,
                ),
            ]
        )

    def swap(w, tot, total):
        state = [halves(x) for x in (tops[w], tot, total)]
        for row, pair in enumerate(state):
            swap_stat_out[w, row : row + 1, :] = pair[w]
            comb_stat_out[w, row : row + 1, :] = pair[1 - w]
        swap_out[w] = acc[w, :, pl.ds(w * n_q, n_q)].astype(jnp.bfloat16)
        for copy in swaps[w]:
            copy.start()

    def add_up(w):
        mine = [comb_stat_out[w, row : row + 1, :] for row in range(3)]
        theirs = [swap_stat_in[w, row : row + 1, :] for row in range(3)]
        best = jnp.maximum(mine[0], theirs[0])
        factors = [jnp.exp2((x[0] - best) * (scale * LOG2E)) for x in (mine, theirs)]
        comb_out[w] = (
            acc[w, :, pl.ds((1 - w) * n_q, n_q)] * factors[0]
            + swap_in[w].astype(jnp.float32) * factors[1]
        ).astype(jnp.bfloat16)
        comb_stat_out[w, 0:1, :] = best
        comb_stat_out[w, 1:2, :] = mine[1] * factors[0] + theirs[1] * factors[1]
        comb_stat_out[w, 2:3, :] = mine[2] + theirs[2]
        for copy in combs[w]:
            copy.start()

    swap(0, *parts_pass(0, tops[0], acc.at[0], 0, 1))
    parts_pass(1, tops[1], acc.at[1], 0, 2)
    early = lax.rem(me, 4) < 2

    @pl.when(early)
    def _():
        for copy in swaps[0]:
            copy.wait_recv()
        add_up(0)

    swap(1, *parts_pass(1, tops[1], acc.at[1], 1, 2))

    @pl.when(jnp.logical_not(early))
    def _():
        for copy in swaps[0]:
            copy.wait_recv()
        add_up(0)

    for copy in swaps[1]:
        copy.wait_recv()
    add_up(1)

    for w in range(2):
        for copy in combs[w]:
            copy.wait_recv()
        far = [comb_stat_in[w, row : row + 1, :] for row in range(3)]
        best = jnp.maximum(own_top[w], far[0])
        factors = [jnp.exp2((x - best) * (scale * LOG2E)) for x in (own_top[w], far[0])]
        mass = factors[0] * own_tot[w] + factors[1] * far[1]
        best_ref[w : w + 1, :] = best * scale
        log_ref[w : w + 1, :] = jnp.log(mass)
        total_ref[w : w + 1, :] = (own_sum[w] + far[2]) * scale
        size_ref[w : w + 1, :] = own_bounds[w][1].astype(jnp.float32)
        pooled = acc_own[:, w * n_q : (w + 1) * n_q] * (factors[0] / mass)
        pooled += comb_in[w].astype(jnp.float32) * (factors[1] / mass)
        pooled_ref[:, pl.ds(w * dim, dim)] = pooled.astype(jnp.bfloat16).T

    for copy in q_copies + swaps[0] + swaps[1] + combs[0] + combs[1]:
        copy.wait_send()


def solution(mesh):
    n_dev = mesh.shape["tm"] * mesh.shape["pb"]
    n_pb = mesh.shape["pb"]

    def local(queries, corpus, window_start, window_end):
        n_q, dim = queries.shape
        n_doc = corpus.shape[0]
        scale = SCORE_SCALE / math.sqrt(dim)
        any_spec = pl.BlockSpec(memory_space=pltpu.HBM)
        vmem_spec = pl.BlockSpec(memory_space=pltpu.VMEM)
        dma = pltpu.SemaphoreType.DMA
        row = jax.ShapeDtypeStruct((2, n_q), jnp.float32)
        pooled, best, log, total, size = pl.pallas_call(
            functools.partial(kernel, n_dev, n_pb, scale),
            out_shape=(jax.ShapeDtypeStruct((n_q, 2 * dim), jnp.bfloat16),) + (row,) * 4,
            in_specs=[any_spec] * 4,
            out_specs=(vmem_spec,) * 5,
            scratch_shapes=[
                pltpu.VMEM((n_doc, dim), jnp.bfloat16),
                pltpu.VMEM((dim, n_doc), jnp.bfloat16),
                pltpu.VMEM((2, n_doc, 2 * n_q), jnp.float32),
                pltpu.VMEM((n_q, dim), jnp.bfloat16),
                pltpu.VMEM((2, n_q, dim), jnp.bfloat16),
                pltpu.VMEM((dim, 2 * n_q), jnp.bfloat16),
                pltpu.VMEM((2, 2, n_q), jnp.int32),
                pltpu.VMEM((2, 2, 2, n_q), jnp.int32),
                pltpu.VMEM((2, 8, 2 * n_q), jnp.float32),
                pltpu.VMEM((8, 2 * n_q), jnp.float32),
                pltpu.VMEM((8, 2 * n_q), jnp.float32),
                pltpu.VMEM((2, dim, 2 * n_q), jnp.float32),
                pltpu.VMEM((dim, 2 * n_q), jnp.float32),
                pltpu.VMEM((2, dim, n_q), jnp.bfloat16),
                pltpu.VMEM((2, dim, n_q), jnp.bfloat16),
                pltpu.VMEM((2, dim, n_q), jnp.bfloat16),
                pltpu.VMEM((2, dim, n_q), jnp.bfloat16),
                pltpu.VMEM((2, 8, n_q), jnp.float32),
                pltpu.VMEM((2, 8, n_q), jnp.float32),
                pltpu.VMEM((2, 8, n_q), jnp.float32),
                pltpu.VMEM((2, 8, n_q), jnp.float32),
                dma((n_doc // COPY_ROWS,)),
                dma((3,)),
                dma((2,)),
                dma((2,)),
                dma((2,)),
                dma((2,)),
                dma((2, 2)),
                dma((2, 2)),
                dma((2, 2)),
                dma((2, 2)),
            ],
            compiler_params=pltpu.CompilerParams(
                collective_id=0,
                has_side_effects=True,
                vmem_limit_bytes=62 * 1024 * 1024,
            ),
            name="window_pool",
        )(queries, corpus, window_start.T, window_end.T)
        return pooled.reshape(n_q, 2, dim), (best + log).T, (total / size).T

    rows = P(("tm", "pb"), None)
    return jax.shard_map(
        local,
        mesh=mesh,
        in_specs=(rows,) * 4,
        out_specs=(P(("tm", "pb"), None, None), rows, rows),
        check_vma=False,
    )
```

time: 52 us -> 47.3 us (0.910)
  the two profiles are of different devices: /device:TPU:1 before, /device:TPU:4 now
where the time goes in v2:
time: 47.3 us; the launch traced here: 47.2 us
  Pallas kernels  43.4 us (92%)
  local copies, waits for them, and re-layouts  1.83 us (4%)
  other arithmetic  1.27 us (3%)
  between operations  0.64 us (1%)
    pallas_call x1, Pallas kernels, local(): pl.pallas_call(functools.partial(kernel, n_dev, n_pb, scale), out_shape=(...  43.4 us
    reshape x1, local copies, waits for them, and re-layouts, local(): return (pooled.reshape(n_q, 2, dim), (best + log).T, (total / size).T)  1.83 us
    transpose x1, other arithmetic, local(): return (pooled.reshape(n_q, 2, dim), (best + log).T, (total / size).T)  1.27 us

profile of v2, /device:TPU:4, one launch (start us, length us, event | category | flops | bytes accessed | tf_op | source)
XLA Modules:
  0.0 47.2 jit_solution(8678289811980548825)
XLA Ops:
  0.6 43.4 %window_pool.1 = (bf16[128,1536]{1,0:T(8,128)(2,1)}, f32[2,128]{1,0:T(2,128)}, f32[2,128]{1,0:T(2,128)}, f32[2,128]{1,0:T(2,128)}, f32[2,128]{1,0:T(2,128)}) custom-call(bf16[128,768]{1,0:T(8,128)(2,1)} %q_hbm.1, bf16[8192,768]{1,0:T(8,128)(2,1)} %c_hbm.1, s32[2,128]{1,0:T(2,128)} %bitcast.6, s32[2,128]{1,0:T(2,128)} %bitcast.7), custom_call_target="tpu_custom_call" | custom-call | tf_op jit(solution)/shard_map/window_pool/pallas_call | solution.py:309
  44.1 1.3 %add_bitcast_fusion = (f32[128,2]{0,1:T(2,128)}, f32[128,2]{0,1:T(2,128)}) fusion(f32[2,128]{1,0:T(2,128)} %get-tuple-element.9, f32[2,128]{1,0:T(2,128)} %get-tuple-element.10, f32[2,128]{1,0:T(2,128)} %get-tuple-element.11, f32[2,128]{1,0:T(2,128)} %get-tuple-element.12), kind=kLoop, calls=%fused_computation | loop fusion | flops 512 | bytes 6144 | tf_op jit(solution)/shard_map/transpose | solution.py:354
  45.3 1.8 %reshape.9 = bf16[128,2,768]{2,1,0:T(2,128)(2,1)} reshape(bf16[128,1536]{1,0:T(8,128)(2,1)} %get-tuple-element.8) | data formatting | bytes 786432 | tf_op jit(solution)/shard_map/reshape | solution.py:354

commit v3 on v2

--- a/solution.py
+++ b/solution.py
@@ -13,6 +13,7 @@
 LOG2E = math.log2(math.e)
 MESH = pl.DeviceIdType.MESH
 
+LINE = 32
 COPY_ROWS = 1024
 OWN_ROWS = 2048
 ROWS = 2048
@@ -27,6 +28,7 @@
 def kernel(
     n_dev,
     n_pb,
+    line,
     scale,
     q_hbm,
     c_hbm,
@@ -58,6 +60,9 @@
     swap_stat_in,
     comb_stat_out,
     comb_stat_in,
+    far_in,
+    far_stat_in,
+    far_sum,
     c_sem,
     local_sem,
     q_send,
@@ -68,6 +73,7 @@
     swap_recv,
     comb_send,
     comb_recv,
+    far_recv,
 ):
     n_q, dim = q_hbm.shape
     n_doc = c_hbm.shape[0]
@@ -99,20 +105,41 @@
     stop_copy.start()
     lax.fori_loop(0, n_doc // COPY_ROWS, lambda i, _: (c_copy(i).start(), 0)[1], 0)
 
+    def in_array(step):
+        return jnp.logical_and(me + step >= 0, me + step < n_dev)
+
+    def same_line(step):
+        return jnp.logical_and(in_array(step), (me + n_dev) // line == (me + n_dev + step) // line)
+
+    peers = {-2: same_line(-2), -1: in_array(-1), 1: in_array(1), 2: same_line(2)}
     barrier = pltpu.get_barrier_semaphore()
-    for step in (-2, -1, 1, 2):
-        pl.semaphore_signal(barrier, inc=1, device_id=device(step), device_id_type=MESH)
-    pl.semaphore_wait(barrier, 4)
+    for step, there in peers.items():
+
+        @pl.when(there)
+        def _(step=step):
+            pl.semaphore_signal(barrier, inc=1, device_id=device(step), device_id_type=MESH)
+
+    pl.semaphore_wait(barrier, sum(there.astype(jnp.int32) for there in peers.values()))
     q_copy.wait()
     start_copy.wait()
     stop_copy.wait()
 
-    q_copies = []
+    q_copies = [[], []]
     for slot, step in ((1, -1), (0, 1)):
-        q_copies.append(send(w_v, w_in.at[slot], w_send.at[slot], w_recv.at[slot], step))
-        q_copies.append(send(q_v, q_in.at[slot], q_send.at[slot], q_recv.at[slot], step))
-    for copy in q_copies:
-        copy.start()
+        q_copies[slot] = [
+            send(w_v, w_in.at[slot], w_send.at[slot], w_recv.at[slot], step),
+            send(q_v, q_in.at[slot], q_send.at[slot], q_recv.at[slot], step),
+        ]
+
+        @pl.when(peers[step])
+        def _(slot=slot):
+            for copy in q_copies[slot]:
+                copy.start()
+
+        @pl.when(jnp.logical_not(peers[step]))
+        def _(slot=slot):
+            q_in[1 - slot] = q_v[...]
+            w_in[1 - slot] = w_v[...]
 
     start_doc = me * n_doc
 
@@ -188,8 +215,13 @@
         halves, parts_pass(0, jnp.concatenate(own_top, axis=1), acc_own, 0, 1)
     )
 
-    for copy in q_copies:
-        copy.wait_recv()
+    for slot, step in ((0, -1), (1, 1)):
+
+        @pl.when(peers[step])
+        def _(slot=slot):
+            for copy in q_copies[slot]:
+                copy.wait_recv()
+
     for slot in range(2):
         q_t[:, pl.ds(slot * n_q, n_q)] = q_in[slot].T
     bounds = []
@@ -199,35 +231,45 @@
         bounds.append((low - start_doc, stop - low))
     tops = scores_pass(q_t, bounds, (0, 1), (pl.ds(0, 2 * n_q),) * 2, ROWS, False)
 
-    swaps, combs = [], []
+    swaps, combs, straights, fars = [], [], [], []
+
+    def state_copies(out, stat_out, into, stat_into, sems, w, step):
+        return [
+            send(out.at[w], into.at[w], sems[0].at[w, 0], sems[1].at[w, 0], step),
+            send(stat_out.at[w], stat_into.at[w], sems[0].at[w, 1], sems[1].at[w, 1], step),
+        ]
+
+    into_comb = (comb_in, comb_stat_in)
+    into_far = (far_in, far_stat_in)
     for w in range(2):
         swap_step, comb_step = ((-2, 1), (2, -1))[w]
-        sem = (swap_send, swap_recv)
+        from_swap = (swap_out, swap_stat_out)
+        from_comb = (comb_out, comb_stat_out)
+        swap_sems, comb_sems = (swap_send, swap_recv), (comb_send, comb_recv)
+        owner_sems, far_sems = (swap_send, comb_recv), (swap_send, far_recv)
         swaps.append(
-            [
-                send(swap_out.at[w], swap_in.at[w], sem[0].at[w, 0], sem[1].at[w, 0], swap_step),
-                send(
-                    swap_stat_out.at[w],
-                    swap_stat_in.at[w],
-                    sem[0].at[w, 1],
-                    sem[1].at[w, 1],
-                    swap_step,
-                ),
-            ]
+            state_copies(*from_swap, swap_in, swap_stat_in, swap_sems, w, swap_step)
         )
-        sem = (comb_send, comb_recv)
-        combs.append(
-            [
-                send(comb_out.at[w], comb_in.at[w], sem[0].at[w, 0], sem[1].at[w, 0], comb_step),
-                send(
-                    comb_stat_out.at[w],
-                    comb_stat_in.at[w],
-                    sem[0].at[w, 1],
-                    sem[1].at[w, 1],
-                    comb_step,
-                ),
-            ]
+        combs.append(state_copies(*from_comb, *into_comb, comb_sems, w, comb_step))
+        straights.append(state_copies(*from_swap, *into_comb, owner_sems, w, swap_step // 2))
+        fars.append(
+            (
+                state_copies(*from_swap, *into_far, far_sems, w, swap_step // 2),
+                state_copies(*from_comb, *into_far, (comb_send, far_recv), w, comb_step),
+            )
         )
+
+    def start(copies, when):
+        @pl.when(when)
+        def _():
+            for copy in copies:
+                copy.start()
+
+    def wait_recv(copies, when):
+        @pl.when(when)
+        def _():
+            for copy in copies:
+                copy.wait_recv()
 
     def swap(w, tot, total):
         state = [halves(x) for x in (tops[w], tot, total)]
@@ -235,50 +277,86 @@
             swap_stat_out[w, row : row + 1, :] = pair[w]
             comb_stat_out[w, row : row + 1, :] = pair[1 - w]
         swap_out[w] = acc[w, :, pl.ds(w * n_q, n_q)].astype(jnp.bfloat16)
-        for copy in swaps[w]:
-            copy.start()
+        far_step = (-2, 2)[w]
+        owner_step = far_step // 2
+        start(swaps[w], peers[far_step])
+        near = jnp.logical_and(same_line(owner_step), jnp.logical_not(peers[far_step]))
+        start(straights[w], near)
+        start(fars[w][0], jnp.logical_and(peers[owner_step], jnp.logical_not(same_line(owner_step))))
 
     def add_up(w):
+        paired = peers[(2, -2)[w]]
+        owner_step = (1, -1)[w]
         mine = [comb_stat_out[w, row : row + 1, :] for row in range(3)]
-        theirs = [swap_stat_in[w, row : row + 1, :] for row in range(3)]
-        best = jnp.maximum(mine[0], theirs[0])
-        factors = [jnp.exp2((x[0] - best) * (scale * LOG2E)) for x in (mine, theirs)]
-        comb_out[w] = (
-            acc[w, :, pl.ds((1 - w) * n_q, n_q)] * factors[0]
-            + swap_in[w].astype(jnp.float32) * factors[1]
-        ).astype(jnp.bfloat16)
-        comb_stat_out[w, 0:1, :] = best
-        comb_stat_out[w, 1:2, :] = mine[1] * factors[0] + theirs[1] * factors[1]
-        comb_stat_out[w, 2:3, :] = mine[2] + theirs[2]
-        for copy in combs[w]:
-            copy.start()
+        mine_part = pl.ds((1 - w) * n_q, n_q)
+
+        @pl.when(paired)
+        def _():
+            for copy in swaps[w]:
+                copy.wait_recv()
+            theirs = [swap_stat_in[w, row : row + 1, :] for row in range(3)]
+            best = jnp.maximum(mine[0], theirs[0])
+            factors = [jnp.exp2((x[0] - best) * (scale * LOG2E)) for x in (mine, theirs)]
+            comb_out[w] = (
+                acc[w, :, mine_part] * factors[0] + swap_in[w].astype(jnp.float32) * factors[1]
+            ).astype(jnp.bfloat16)
+            comb_stat_out[w, 0:1, :] = best
+            comb_stat_out[w, 1:2, :] = mine[1] * factors[0] + theirs[1] * factors[1]
+            comb_stat_out[w, 2:3, :] = mine[2] + theirs[2]
+
+        @pl.when(jnp.logical_not(paired))
+        def _():
+            comb_out[w] = acc[w, :, mine_part].astype(jnp.bfloat16)
+
+        start(combs[w], same_line(owner_step))
+        start(
+            fars[w][1], jnp.logical_and(peers[owner_step], jnp.logical_not(same_line(owner_step)))
+        )
 
     swap(0, *parts_pass(0, tops[0], acc.at[0], 0, 1))
+    early = jnp.logical_or(lax.rem(me, 4) < 2, jnp.logical_not(peers[2]))
     parts_pass(1, tops[1], acc.at[1], 0, 2)
-    early = lax.rem(me, 4) < 2
 
     @pl.when(early)
     def _():
-        for copy in swaps[0]:
-            copy.wait_recv()
         add_up(0)
 
     swap(1, *parts_pass(1, tops[1], acc.at[1], 1, 2))
 
     @pl.when(jnp.logical_not(early))
     def _():
-        for copy in swaps[0]:
-            copy.wait_recv()
         add_up(0)
 
-    for copy in swaps[1]:
-        copy.wait_recv()
     add_up(1)
 
+    edge = jnp.logical_or(
+        jnp.logical_and(peers[-1], jnp.logical_not(same_line(-1))),
+        jnp.logical_and(peers[1], jnp.logical_not(same_line(1))),
+    )
     for w in range(2):
-        for copy in combs[w]:
-            copy.wait_recv()
-        far = [comb_stat_in[w, row : row + 1, :] for row in range(3)]
+        wait_recv(combs[w], me >= 0)
+        wait_recv(fars[w][1], edge)
+
+        @pl.when(edge)
+        def _(w=w):
+            mine = [comb_stat_in[w, row : row + 1, :] for row in range(3)]
+            theirs = [far_stat_in[w, row : row + 1, :] for row in range(3)]
+            best = jnp.maximum(mine[0], theirs[0])
+            factors = [jnp.exp2((x[0] - best) * (scale * LOG2E)) for x in (mine, theirs)]
+            acc[w, :, pl.ds(0, n_q)] = (
+                comb_in[w].astype(jnp.float32) * factors[0]
+                + far_in[w].astype(jnp.float32) * factors[1]
+            )
+            far_sum[w, 0:1, :] = best
+            far_sum[w, 1:2, :] = mine[1] * factors[0] + theirs[1] * factors[1]
+            far_sum[w, 2:3, :] = mine[2] + theirs[2]
+
+        @pl.when(jnp.logical_not(edge))
+        def _(w=w):
+            acc[w, :, pl.ds(0, n_q)] = comb_in[w].astype(jnp.float32)
+            far_sum[w] = comb_stat_in[w]
+
+        far = [far_sum[w, row : row + 1, :] for row in range(3)]
         best = jnp.maximum(own_top[w], far[0])
         factors = [jnp.exp2((x - best) * (scale * LOG2E)) for x in (own_top[w], far[0])]
         mass = factors[0] * own_tot[w] + factors[1] * far[1]
@@ -287,11 +365,23 @@
         total_ref[w : w + 1, :] = (own_sum[w] + far[2]) * scale
         size_ref[w : w + 1, :] = own_bounds[w][1].astype(jnp.float32)
         pooled = acc_own[:, w * n_q : (w + 1) * n_q] * (factors[0] / mass)
-        pooled += comb_in[w].astype(jnp.float32) * (factors[1] / mass)
+        pooled += acc[w, :, pl.ds(0, n_q)] * (factors[1] / mass)
         pooled_ref[:, pl.ds(w * dim, dim)] = pooled.astype(jnp.bfloat16).T
 
-    for copy in q_copies + swaps[0] + swaps[1] + combs[0] + combs[1]:
-        copy.wait_send()
+    for slot, step in ((1, -1), (0, 1)):
+
+        @pl.when(peers[step])
+        def _(slot=slot):
+            for copy in q_copies[slot]:
+                copy.wait_send()
+
+    for w in range(2):
+        for copies, step in ((swaps[w], (-1, 1)[w]), (combs[w], (1, -1)[w])):
+
+            @pl.when(peers[step])
+            def _(copies=copies):
+                for copy in copies:
+                    copy.wait_send()
 
 
 def solution(mesh):
@@ -307,7 +397,7 @@
         dma = pltpu.SemaphoreType.DMA
         row = jax.ShapeDtypeStruct((2, n_q), jnp.float32)
         pooled, best, log, total, size = pl.pallas_call(
-            functools.partial(kernel, n_dev, n_pb, scale),
+            functools.partial(kernel, n_dev, n_pb, min(LINE, n_dev), scale),
             out_shape=(jax.ShapeDtypeStruct((n_q, 2 * dim), jnp.bfloat16),) + (row,) * 4,
             in_specs=[any_spec] * 4,
             out_specs=(vmem_spec,) * 5,
@@ -333,12 +423,16 @@
                 pltpu.VMEM((2, 8, n_q), jnp.float32),
                 pltpu.VMEM((2, 8, n_q), jnp.float32),
                 pltpu.VMEM((2, 8, n_q), jnp.float32),
+                pltpu.VMEM((2, dim, n_q), jnp.bfloat16),
+                pltpu.VMEM((2, 8, n_q), jnp.float32),
+                pltpu.VMEM((2, 8, n_q), jnp.float32),
                 dma((n_doc // COPY_ROWS,)),
                 dma((3,)),
                 dma((2,)),
                 dma((2,)),
                 dma((2,)),
                 dma((2,)),
+                dma((2, 2)),
                 dma((2, 2)),
                 dma((2, 2)),
                 dma((2, 2)),

time: 47.3 us -> 42.6 us (0.901); the launches traced: 47.2 us -> 41.8 us
  Pallas kernels: 43.4 us -> 38.1 us
    pallas_call x1, Pallas kernels: 43.4 us -> 38.1 us  [local(): pl.pallas_call(functools.partial(kernel, n_dev, n_pb, min(LINE, n_dev), s...]
where the time goes in v3:
time: 42.6 us; the launch traced here: 41.8 us
  Pallas kernels  38.1 us (89%)
  local copies, waits for them, and re-layouts  1.83 us (4%)
  other arithmetic  1.27 us (3%)
  between operations  0.64 us (2%)
    pallas_call x1, Pallas kernels, local(): pl.pallas_call(functools.partial(kernel, n_dev, n_pb, min(LINE, n_dev), s...  38.1 us
    reshape x1, local copies, waits for them, and re-layouts, local(): return (pooled.reshape(n_q, 2, dim), (best + log).T, (total / size).T)  1.83 us
    transpose x1, other arithmetic, local(): return (pooled.reshape(n_q, 2, dim), (best + log).T, (total / size).T)  1.27 us

profile of v3, /device:TPU:4, one launch (start us, length us, event | category | flops | bytes accessed | tf_op | source)
XLA Modules:
  0.0 41.8 jit_solution(7359710759407015550)
XLA Ops:
  0.6 38.1 %window_pool.1 = (bf16[128,1536]{1,0:T(8,128)(2,1)}, f32[2,128]{1,0:T(2,128)}, f32[2,128]{1,0:T(2,128)}, f32[2,128]{1,0:T(2,128)}, f32[2,128]{1,0:T(2,128)}) custom-call(bf16[128,768]{1,0:T(8,128)(2,1)} %q_hbm.1, bf16[8192,768]{1,0:T(8,128)(2,1)} %c_hbm.1, s32[2,128]{1,0:T(2,128)} %bitcast.6, s32[2,128]{1,0:T(2,128)} %bitcast.7), custom_call_target="tpu_custom_call" | custom-call | tf_op jit(solution)/shard_map/window_pool/pallas_call | solution.py:399
  38.7 1.3 %add_bitcast_fusion = (f32[128,2]{0,1:T(2,128)}, f32[128,2]{0,1:T(2,128)}) fusion(f32[2,128]{1,0:T(2,128)} %get-tuple-element.9, f32[2,128]{1,0:T(2,128)} %get-tuple-element.10, f32[2,128]{1,0:T(2,128)} %get-tuple-element.11, f32[2,128]{1,0:T(2,128)} %get-tuple-element.12), kind=kLoop, calls=%fused_computation | loop fusion | flops 512 | bytes 6144 | tf_op jit(solution)/shard_map/transpose | solution.py:448
  40.0 1.8 %reshape.9 = bf16[128,2,768]{2,1,0:T(2,128)(2,1)} reshape(bf16[128,1536]{1,0:T(8,128)(2,1)} %get-tuple-element.8) | data formatting | bytes 786432 | tf_op jit(solution)/shard_map/reshape | solution.py:448
